TPU v7x, 32 devices: a whole 2x2x4 slice. The times are simulated.
32 devices in a mesh: seq: 8 (over z, y), head: 4 (over x, core).
Axes of the slice: x: 2, y: 2, z: 4, core: 2. Of those that a mesh axis runs over, the one named last changes fastest.
Arguments:
- queries: bfloat16 [2048, 4096], P(('seq', 'head')), may hold values from -9 to 9, as said below
- keys: bfloat16 [2048, 512], P(('seq', 'head')), may hold values from -9 to 9, as said below
- values: bfloat16 [2048, 512], P(('seq', 'head')), may hold values from -6 to 6
Outputs:
- attended: bfloat16 [2048, 4096], P(('seq', 'head'))
Inputs may be any that keep to these rules, and one draw needn't show every extreme that they name: `queries`: query entries are of order one except on a few rows. `keys`: key entries are of order one except on a few rows.
All inputs are finite; a program needn't handle non-finite values.
Results may differ from a plain program's by a relative error of at most 0.005.
Values may be sent and summed in bfloat16 or wider, within the bound.
A program may use at most 64 MiB of HBM per device.

v0:
```python
import math

import jax
import jax.numpy as jnp
from jax import lax
from jax.sharding import PartitionSpec as P

H = 32
KV = 4
DH = 128


def per_device(queries, keys, values):
    n_head = lax.axis_size("head")
    tok = queries.shape[0]
    per_dev = H // n_head
    group = tok * n_head
    scale = 1.0 / math.sqrt(DH)
    me_seq = lax.axis_index("seq")
    arranged = queries.reshape(tok, n_head, per_dev * DH)
    received = lax.all_to_all(arranged, "head", split_axis=1, concat_axis=0, tiled=True)
    mine = received.reshape(group, per_dev, DH)
    first = me_seq * group
    last = first + group - 1
    query_pos = first + jnp.arange(group, dtype=jnp.int32)
    init = (
        jnp.full((group, per_dev), -1e30, jnp.float32),
        jnp.zeros((group, per_dev), jnp.float32),
        jnp.zeros((group, per_dev, DH), jnp.float32),
    )
    wide_keys = jnp.repeat(keys.reshape(tok, KV, DH), n_head // KV, axis=1)
    wide_values = jnp.repeat(values.reshape(tok, KV, DH), n_head // KV, axis=1)
    slot_keys, slot_values = (
        lax.all_to_all(wide_keys, "head", split_axis=1, concat_axis=0, tiled=True),
        lax.all_to_all(wide_values, "head", split_axis=1, concat_axis=0, tiled=True),
    )
    k_piece = lax.all_gather(slot_keys.reshape(group, DH), "seq", axis=0, tiled=True)
    v_piece = lax.all_gather(slot_values.reshape(group, DH), "seq", axis=0, tiled=True)
    rows = k_piece.shape[0]
    width = math.gcd(rows, 512)

    def step(index, state):
        block_start = index * width

        def work(inner):
            running, total, acc = inner
            k_blk = lax.dynamic_slice_in_dim(k_piece, index * width, width, 0)
            v_blk = lax.dynamic_slice_in_dim(v_piece, index * width, width, 0)
            scores = (
                jnp.einsum("ghd,kd->ghk", mine, k_blk, preferred_element_type=jnp.float32) * scale
            )
            key_pos = block_start + jnp.arange(width, dtype=jnp.int32)
            scores = jnp.where(key_pos[None, None, :] <= query_pos[:, None, None], scores, -jnp.inf)
            newmax = jnp.maximum(running, jnp.max(scores, axis=2))
            factor = jnp.exp(running - newmax)
            expo = jnp.exp(scores - newmax[:, :, None])
            total = factor * total + jnp.sum(expo, axis=2)
            acc = factor[:, :, None] * acc + jnp.einsum(
                "ghk,kd->ghd", expo.astype(jnp.bfloat16), v_blk, preferred_element_type=jnp.float32
            )
            return (newmax, total, acc)

        def skip(inner):
            return inner

        return lax.cond(block_start <= last, work, skip, state)

    state = lax.fori_loop(0, rows // width, step, init)
    running, total, acc = state
    output = (acc / total[:, :, None]).astype(jnp.bfloat16)
    output = output.reshape(group, 1, per_dev * DH)
    returned = lax.all_to_all(output, "head", split_axis=0, concat_axis=1, tiled=True)
    return returned.reshape(tok, H * DH)


def solution(mesh):
    in_specs = (P(("seq", "head"), None), P(("seq", "head"), None), P(("seq", "head"), None))
    out_specs = P(("seq", "head"), None)
    return jax.shard_map(
        per_device, mesh=mesh, in_specs=in_specs, out_specs=out_specs, check_vma=False
    )
```

profile of v0, /device:TPU:28, one launch (start us, length us, event | category | flops | bytes accessed | tf_op | source)
XLA Modules:
  0.0 113.0 jit_solution(6079941349472919362)
XLA Ops:
  1.5 3.3 %all-to-all-start = ((bf16[64,4,128]{2,0,1:T(8,128)(2,1)}), bf16[64,4,128]{2,0,1:T(8,128)(2,1)S(1)}, u32[]{:S(2)}, u32[]{:S(2)}) async-start(bf16[64,4,128]{2,0,1:T(8,128)(2,1)} %copy_bitcast_fusion.2), calls=%async_computation | async-start | bytes 131072 | tf_op jit(solution)/shard_map/all_to_all | solution.py:34
  4.8 1.5 %copy_bitcast_fusion.1 = bf16[64,4,128]{2,0,1:T(8,128)(2,1)} fusion(bf16[64,512]{1,0:T(8,128)(2,1)} %param.9), kind=kLoop, calls=%fused_computation.25 | loop fusion | bytes 131072 | tf_op jit(solution)/shard_map/reshape;broadcast_in_dim;reshape | solution.py:32
  6.2 2.6 %all-to-all-done = bf16[64,4,128]{2,0,1:T(8,128)(2,1)S(1)} async-done(((bf16[64,4,128]{2,0,1:T(8,128)(2,1)}), bf16[64,4,128]{2,0,1:T(8,128)(2,1)S(1)}, u32[]{:S(2)}, u32[]{:S(2)}) %all-to-all-start) | async-done | bytes 65568 | tf_op jit(solution)/shard_map/all_to_all | solution.py:34
  8.9 3.3 %all-to-all-start.2 = ((bf16[64,4,128]{2,0,1:T(8,128)(2,1)}), bf16[64,4,128]{2,0,1:T(8,128)(2,1)S(1)}, u32[]{:S(2)}, u32[]{:S(2)}) async-start(bf16[64,4,128]{2,0,1:T(8,128)(2,1)} %copy_bitcast_fusion.1), calls=%async_computation.2 | async-start | bytes 131072 | tf_op jit(solution)/shard_map/all_to_all | solution.py:35
  12.2 1.9 %copy.40 = bf16[8,4,8,1024]{3,2,0,1:T(8,128)(2,1)} copy(bf16[8,4,8,1024]{3,2,1,0:T(8,128)(2,1)} %bitcast.65) | data formatting | bytes 1048576 | tf_op jit(solution)/shard_map/reshape | solution.py:20
  14.0 2.2 %all-to-all-done.2 = bf16[64,4,128]{2,0,1:T(8,128)(2,1)S(1)} async-done(((bf16[64,4,128]{2,0,1:T(8,128)(2,1)}), bf16[64,4,128]{2,0,1:T(8,128)(2,1)S(1)}, u32[]{:S(2)}, u32[]{:S(2)}) %all-to-all-start.2) | async-done | bytes 65568 | tf_op jit(solution)/shard_map/all_to_all | solution.py:35
  16.2 3.5 %all-to-all-start.1 = ((bf16[64,4,1024]{2,0,1:T(8,128)(2,1)}), bf16[64,4,1024]{2,0,1:T(8,128)(2,1)S(1)}, u32[]{:S(2)}, u32[]{:S(2)}) async-start(bf16[64,4,1024]{2,0,1:T(8,128)(2,1)} %bitcast.59), calls=%async_computation.1 | async-start | bytes 1048576 | tf_op jit(solution)/shard_map/all_to_all | solution.py:21
  19.7 31.4 %all_gather.6 = bf16[2048,128]{1,0:T(8,128)(2,1)S(1)} all-gather(bf16[256,128]{1,0:T(8,128)(2,1)S(1)} %bitcast.66), channel_id=1, replica_groups=mesh['seq'=8,'head'=4] {'seq'}, dimensions={0}, use_global_device_ids=true | all-gather | bytes 589824 | tf_op jit(solution)/shard_map/all_gather | solution.py:37
  51.1 31.6 %all_gather.7 = bf16[2048,128]{1,0:T(8,128)(2,1)S(1)} all-gather(bf16[256,128]{1,0:T(8,128)(2,1)S(1)} %bitcast.67), channel_id=1, replica_groups=mesh['seq'=8,'head'=4] {'seq'}, dimensions={0}, use_global_device_ids=true | all-gather | bytes 589824 | tf_op jit(solution)/shard_map/all_gather | solution.py:38
  83.0 13.5 %while.18 = (s32[]{:T(128)}, f32[256,8]{0,1:T(8,128)S(1)}, f32[256,8]{0,1:T(8,128)S(1)}, f32[256,8,128]{2,0,1:T(8,128)S(1)}, s32[]{:T(128)}, /*index=5*/bf16[204...) while((s32[]{:T(128)}, f32[256,8]{0,1:T(8,128)S(1)}, ...), condition=%wide.region_5.6_spmd.clone, body=%wide.region_0.5_spmd.clone.sunk | while | flops 549065472 | bytes 16130381 | solution.py:68
  83.0 3.3 %conditional.3 = ((f32[256,8]{0,1:T(8,128)S(1)}, f32[256,8]{0,1:T(8,128)S(1)}, f32[256,8,128]{2,0,1:T(8,128)S(1)})) conditional(s32[]{:T(128)} %convert_element_type.21, (f32[256,8]{0,1:T(8,128)S(1)}, f32[256,8]{0,1:T(8,128)S(1)}, f32[256,8,128]{2,0,1:T(8,128)S(1)}) %tuple.47, (s32[]{:T(128)}, s32[]{:T(128)}, s32[]{:T(128)}, ...), branch_computations={%region_1.0_spmd, %region_2.4_spmd} | conditional | flops 549065472 | bytes 16129118 | solution.py:66
  84.0 0.9 fusion.3
  84.9 1.5 %fusion.8 = f32[256,8,128]{2,0,1:T(8,128)S(1)} fusion(f32[512,256,8]{1,0,2:T(8,128)S(1)} %get-tuple-element.279, f32[256,8]{0,1:T(8,128)S(1)} %max.2, pred[256,512]{0,1:T(8,128)(4,1)S(1)} %broadcast_compare_fusion, f32[256,8,128]{2,0,1:T(8,128)S(1)} %get-tuple-element.185, f32[256,8]{0,1:T(8,128)S(1)} %get-tuple-element.277, ...), kind=kOutput, calls=%fused_computation.8 | convolution fusion | flops 273154048 | bytes 6569988 | tf_op jit(solution)/shard_map/while/body/eval_jaxpr/cond/branch_1_fun/ghk,kd->ghd/dot_general | solution.py:58
  86.4 3.3 %conditional.3 = ((f32[256,8]{0,1:T(8,128)S(1)}, f32[256,8]{0,1:T(8,128)S(1)}, f32[256,8,128]{2,0,1:T(8,128)S(1)})) conditional(s32[]{:T(128)} %convert_element_type.21, (f32[256,8]{0,1:T(8,128)S(1)}, f32[256,8]{0,1:T(8,128)S(1)}, f32[256,8,128]{2,0,1:T(8,128)S(1)}) %tuple.47, (s32[]{:T(128)}, s32[]{:T(128)}, s32[]{:T(128)}, ...), branch_computations={%region_1.0_spmd, %region_2.4_spmd} | conditional | flops 549065472 | bytes 16129118 | solution.py:66
  87.4 0.9 fusion.3
  88.3 1.5 %fusion.8 = f32[256,8,128]{2,0,1:T(8,128)S(1)} fusion(f32[512,256,8]{1,0,2:T(8,128)S(1)} %get-tuple-element.279, f32[256,8]{0,1:T(8,128)S(1)} %max.2, pred[256,512]{0,1:T(8,128)(4,1)S(1)} %broadcast_compare_fusion, f32[256,8,128]{2,0,1:T(8,128)S(1)} %get-tuple-element.185, f32[256,8]{0,1:T(8,128)S(1)} %get-tuple-element.277, ...), kind=kOutput, calls=%fused_computation.8 | convolution fusion | flops 273154048 | bytes 6569988 | tf_op jit(solution)/shard_map/while/body/eval_jaxpr/cond/branch_1_fun/ghk,kd->ghd/dot_general | solution.py:58
  89.8 3.3 %conditional.3 = ((f32[256,8]{0,1:T(8,128)S(1)}, f32[256,8]{0,1:T(8,128)S(1)}, f32[256,8,128]{2,0,1:T(8,128)S(1)})) conditional(s32[]{:T(128)} %convert_element_type.21, (f32[256,8]{0,1:T(8,128)S(1)}, f32[256,8]{0,1:T(8,128)S(1)}, f32[256,8,128]{2,0,1:T(8,128)S(1)}) %tuple.47, (s32[]{:T(128)}, s32[]{:T(128)}, s32[]{:T(128)}, ...), branch_computations={%region_1.0_spmd, %region_2.4_spmd} | conditional | flops 549065472 | bytes 16129118 | solution.py:66
  90.8 0.9 fusion.3
  91.7 1.5 %fusion.8 = f32[256,8,128]{2,0,1:T(8,128)S(1)} fusion(f32[512,256,8]{1,0,2:T(8,128)S(1)} %get-tuple-element.279, f32[256,8]{0,1:T(8,128)S(1)} %max.2, pred[256,512]{0,1:T(8,128)(4,1)S(1)} %broadcast_compare_fusion, f32[256,8,128]{2,0,1:T(8,128)S(1)} %get-tuple-element.185, f32[256,8]{0,1:T(8,128)S(1)} %get-tuple-element.277, ...), kind=kOutput, calls=%fused_computation.8 | convolution fusion | flops 273154048 | bytes 6569988 | tf_op jit(solution)/shard_map/while/body/eval_jaxpr/cond/branch_1_fun/ghk,kd->ghd/dot_general | solution.py:58
  93.2 3.3 %conditional.3 = ((f32[256,8]{0,1:T(8,128)S(1)}, f32[256,8]{0,1:T(8,128)S(1)}, f32[256,8,128]{2,0,1:T(8,128)S(1)})) conditional(s32[]{:T(128)} %convert_element_type.21, (f32[256,8]{0,1:T(8,128)S(1)}, f32[256,8]{0,1:T(8,128)S(1)}, f32[256,8,128]{2,0,1:T(8,128)S(1)}) %tuple.47, (s32[]{:T(128)}, s32[]{:T(128)}, s32[]{:T(128)}, ...), branch_computations={%region_1.0_spmd, %region_2.4_spmd} | conditional | flops 549065472 | bytes 16129118 | solution.py:66
  95.0 1.5 %fusion.8 = f32[256,8,128]{2,0,1:T(8,128)S(1)} fusion(f32[512,256,8]{1,0,2:T(8,128)S(1)} %get-tuple-element.279, f32[256,8]{0,1:T(8,128)S(1)} %max.2, pred[256,512]{0,1:T(8,128)(4,1)S(1)} %broadcast_compare_fusion, f32[256,8,128]{2,0,1:T(8,128)S(1)} %get-tuple-element.185, f32[256,8]{0,1:T(8,128)S(1)} %get-tuple-element.277, ...), kind=kOutput, calls=%fused_computation.8 | convolution fusion | flops 273154048 | bytes 6569988 | tf_op jit(solution)/shard_map/while/body/eval_jaxpr/cond/branch_1_fun/ghk,kd->ghd/dot_general | solution.py:58
  97.5 1.0 reduce
  99.1 11.7 %all_to_all.60 = bf16[4,2,32768]{2,1,0:T(2,128)(2,1)S(1)} all-to-all(bf16[4,2,32768]{2,1,0:T(2,128)(2,1)S(1)} %reshape.66), channel_id=1, replica_groups=mesh['seq'=8,'head'=4] {'head'}, dimensions={0} | all-to-all | bytes 1048576 | tf_op jit(solution)/shard_map/all_to_all | solution.py:72
  112.0 1.0 copy.36
  (50 shorter events, 8.9 us)
Async XLA Ops:
  0.0 0.8 copy-start
  1.5 7.4 %all-to-all-start = ((bf16[64,4,128]{2,0,1:T(8,128)(2,1)}), bf16[64,4,128]{2,0,1:T(8,128)(2,1)S(1)}, u32[]{:S(2)}, u32[]{:S(2)}) async-start(bf16[64,4,128]{2,0,1:T(8,128)(2,1)} %copy_bitcast_fusion.2), calls=%async_computation | async-start | bytes 131072 | tf_op jit(solution)/shard_map/all_to_all | solution.py:34
  8.9 7.4 %all-to-all-start.2 = ((bf16[64,4,128]{2,0,1:T(8,128)(2,1)}), bf16[64,4,128]{2,0,1:T(8,128)(2,1)S(1)}, u32[]{:S(2)}, u32[]{:S(2)}) async-start(bf16[64,4,128]{2,0,1:T(8,128)(2,1)} %copy_bitcast_fusion.1), calls=%async_computation.2 | async-start | bytes 131072 | tf_op jit(solution)/shard_map/all_to_all | solution.py:35
  16.2 66.5 %all-to-all-start.1 = ((bf16[64,4,1024]{2,0,1:T(8,128)(2,1)}), bf16[64,4,1024]{2,0,1:T(8,128)(2,1)S(1)}, u32[]{:S(2)}, u32[]{:S(2)}) async-start(bf16[64,4,1024]{2,0,1:T(8,128)(2,1)} %bitcast.59), calls=%async_computation.1 | async-start | bytes 1048576 | tf_op jit(solution)/shard_map/all_to_all | solution.py:21
where the time goes:
time: 113 us
  blocking collectives  74.7 us (66%)
  starting transfers between devices  10 us (9%)
  matrix products  8.88 us (8%)
  local copies, waits for them, and re-layouts  8.57 us (8%)
  other arithmetic  5.24 us (5%)
  waiting for transfers between devices  4.82 us (4%)
    all_gather x1, blocking collectives, per_device(): lax.all_gather(slot_values.reshape(group, DH), 'seq', axis=0, tiled=True)  31.6 us
    all_gather x1, blocking collectives, per_device(): lax.all_gather(slot_keys.reshape(group, DH), 'seq', axis=0, tiled=True)  31.4 us
    all_to_all x1, blocking collectives, per_device(): lax.all_to_all(output, 'head', split_axis=0, concat_axis=1, tiled=True)  11.7 us
    dot_general x4, matrix products, work(): jnp.einsum('ghk,kd->ghd', expo.astype(jnp.bfloat16), v_blk, preferred_ele...  5.88 us
    all_to_all x1, starting transfers between devices, per_device(): lax.all_to_all(arranged, 'head', split_axis=1, concat_axis=0, tiled=True)  3.47 us
    reduce_sum x4, other arithmetic, work(): total = factor * total + jnp.sum(expo, axis=2)  3.45 us
    all_to_all x1, starting transfers between devices, per_device(): lax.all_to_all(wide_keys, 'head', split_axis=1, concat_axis=0, tiled=True)  3.28 us
    all_to_all x1, starting transfers between devices, per_device(): lax.all_to_all(wide_values, 'head', split_axis=1, concat_axis=0, tiled=True)  3.28 us
  transfers between devices with their start and end apart: 3, of which 2 were waited for; matrix products, arithmetic and copies ran while one was open for 3% of the time, Pallas kernels for 0%

commit v1 on v0

v1 whole, which is shorter than its diff:
```python
import functools
import math

import jax
import jax.numpy as jnp
from jax import lax
from jax.experimental import pallas as pl
from jax.experimental.pallas import tpu as pltpu
from jax.sharding import PartitionSpec as P

H = 32
KV = 4
DH = 128
GROUP = H // KV
PLANE = 8
Z, X, Y, DK, DV, C0 = 0, 1, 2, 3, 4, 5
KINDS = C0 + 4


def kernel(n_head, planes, q_hbm, k_hbm, v_hbm, o_ref, kv, q, mx, acc, lsem, send, recv):
    tok = k_hbm.shape[0]
    me = lax.axis_index("seq") * n_head + lax.axis_index("head")
    core = lax.rem(me, 2)
    x = lax.rem(lax.div(me, 2), 2)
    y = lax.rem(lax.div(me, 4), 2)
    z = lax.div(me, PLANE)

    def dev(linear):
        return (lax.div(linear, n_head), lax.rem(linear, n_head))

    to_x = dev(me + 2 - 4 * x)
    to_y = dev(me + 4 - 8 * y)
    to_core = dev(me + 1 - 2 * core)
    up = dev(lax.min(me + PLANE, planes * PLANE - 1))
    down = dev(lax.max(me - PLANE, 0))

    own_k = pltpu.make_async_copy(k_hbm, kv.at[me, 0], lsem.at[0])
    own_v = pltpu.make_async_copy(v_hbm, kv.at[me, 1], lsem.at[1])
    own_q = pltpu.make_async_copy(q_hbm, q, lsem.at[2])
    own_k.start()
    own_v.start()
    own_q.start()

    barrier = pltpu.get_barrier_semaphore()

    def greet(where):
        pl.semaphore_signal(barrier, inc=1, device_id=where, device_id_type=pl.DeviceIdType.MESH)

    greet(to_x)
    greet(to_y)
    greet(to_core)

    @pl.when(z < planes - 1)
    def _():
        greet(up)

    @pl.when(z > 0)
    def _():
        greet(down)

    pl.semaphore_wait(barrier, 3 + lax.min(z, 1) + lax.min(planes - 1 - z, 1))

    own_k.wait()
    own_v.wait()

    def slot(k, yy, xx, cc):
        return (z - k) * PLANE + yy * 4 + xx * 2 + cc

    def copy(kind, k, where, block, half=None, later=0):
        ref = kv.at[block] if half is None else kv.at[block, half]
        return pltpu.make_async_remote_copy(
            src_ref=ref,
            dst_ref=ref,
            send_sem=send.at[kind, k],
            recv_sem=recv.at[kind, k + later],
            device_id=where,
            device_id_type=pl.DeviceIdType.MESH,
        )

    def out_z(k):
        return copy(Z, k, up, slot(k, y, x, core), later=1)

    def outs(k):
        mine, xs, ys, diag = (
            slot(k, y, x, core),
            slot(k, y, 1 - x, core),
            slot(k, 1 - y, x, core),
            slot(k, 1 - y, 1 - x, core),
        )
        return dict(
            x=lambda: copy(X, k, to_x, mine),
            y=lambda: copy(Y, k, to_y, mine),
            c0=lambda: copy(C0, k, to_core, mine),
            dk=lambda: copy(DK, k, to_y, xs, 0),
            c1=lambda: copy(C0 + 1, k, to_core, xs),
            dv=lambda: copy(DV, k, to_x, ys, 1),
            c2=lambda: copy(C0 + 2, k, to_core, ys),
            c3=lambda: copy(C0 + 3, k, to_core, diag),
        )

    def ins(k):
        def landed(kind, block, half=None):
            copy(kind, k, to_x, block, half).wait_recv()

        other = 1 - core
        return dict(
            z=lambda: landed(Z, slot(k, y, x, core)),
            x=lambda: landed(X, slot(k, y, 1 - x, core)),
            y=lambda: landed(Y, slot(k, 1 - y, x, core)),
            dk=lambda: landed(DK, slot(k, 1 - y, 1 - x, core), 0),
            dv=lambda: landed(DV, slot(k, 1 - y, 1 - x, core), 1),
            c0=lambda: landed(C0, slot(k, y, x, other)),
            c1=lambda: landed(C0 + 1, slot(k, y, 1 - x, other)),
            c2=lambda: landed(C0 + 2, slot(k, 1 - y, x, other)),
            c3=lambda: landed(C0 + 3, slot(k, 1 - y, 1 - x, other)),
        )

    def launch(k):
        o = outs(k)

        @pl.when(z < planes - 1)
        def _():
            out_z(k).start()

        o["x"]().start()
        o["y"]().start()
        o["c0"]().start()

    scale = math.log2(math.e) / math.sqrt(DH)
    width = PLANE * tok
    rows = GROUP * tok

    def chunk(k, first):
        base = (z - k) * PLANE
        for g in range(KV):
            cols = slice(g * DH, (g + 1) * DH)
            kk = kv[pl.ds(base, PLANE), 0, :, cols].reshape(width, DH)
            vv = kv[pl.ds(base, PLANE), 1, :, cols].reshape(width, DH)
            vv = jnp.concatenate([vv, jnp.ones_like(vv)], axis=1)
            qq = jnp.concatenate(
                [q[:, (g * GROUP + h) * DH : (g * GROUP + h + 1) * DH] for h in range(GROUP)], axis=0
            )
            s = lax.dot_general(
                qq, kk, (((1,), (1,)), ((), ())), preferred_element_type=jnp.float32
            )
            if first:
                row = lax.rem(lax.broadcasted_iota(jnp.int32, (rows, width), 0), tok)
                col = lax.broadcasted_iota(jnp.int32, (rows, width), 1)
                s = jnp.where(col <= row + lax.rem(me, PLANE) * tok, s, -jnp.inf)
            top = jnp.max(s, axis=1, keepdims=True)
            if not first:
                old = mx[g, :, :1]
                top = jnp.maximum(old, top)
            p = jnp.exp2((s - top) * scale).astype(jnp.bfloat16)
            pv = jnp.dot(p, vv, preferred_element_type=jnp.float32)
            if not first:
                pv += acc[g] * jnp.exp2((old - top) * scale)
            acc[g] = pv
            mx[g] = jnp.broadcast_to(top, (rows, DH))

    def step(k, first):
        i, o = ins(k), outs(k)
        i["x"]()
        o["dk"]().start()
        o["c1"]().start()
        i["y"]()
        o["dv"]().start()
        o["c2"]().start()

        @pl.when(k < z)
        def _():
            ins(k + 1)["z"]()
            launch(k + 1)

        i["dk"]()
        i["dv"]()
        o["c3"]().start()
        for name in ("c0", "c1", "c2", "c3"):
            i[name]()
        chunk(k, first)

    launch(0)
    own_q.wait()
    step(0, True)

    def body(k, carry):
        step(k, False)
        return carry

    lax.fori_loop(1, z + 1, body, 0)

    for g in range(KV):
        out = (acc[g, :, :DH] / acc[g, :, DH:]).astype(o_ref.dtype)
        for h in range(GROUP):
            o_ref[:, (g * GROUP + h) * DH : (g * GROUP + h + 1) * DH] = out[h * tok : (h + 1) * tok]

    def drain(k, carry):
        @pl.when(z < planes - 1)
        def _():
            out_z(k).wait_send()

        for c in outs(k).values():
            c().wait_send()
        return carry

    lax.fori_loop(0, z + 1, drain, 0)


def per_device(queries, keys, values):
    n_head = lax.axis_size("head")
    devices = n_head * lax.axis_size("seq")
    planes = devices // PLANE
    tok = queries.shape[0]
    rows = GROUP * tok
    hbm = pl.BlockSpec(memory_space=pl.ANY)
    return pl.pallas_call(
        functools.partial(kernel, n_head, planes),
        out_shape=jax.ShapeDtypeStruct(queries.shape, queries.dtype),
        in_specs=[hbm] * 3,
        out_specs=pl.BlockSpec(memory_space=pltpu.VMEM),
        scratch_shapes=[
            pltpu.VMEM((devices, 2, tok, KV * DH), jnp.bfloat16),
            pltpu.VMEM(queries.shape, jnp.bfloat16),
            pltpu.VMEM((KV, rows, DH), jnp.float32),
            pltpu.VMEM((KV, rows, 2 * DH), jnp.float32),
            pltpu.SemaphoreType.DMA((3,)),
            pltpu.SemaphoreType.DMA((KINDS, planes)),
            pltpu.SemaphoreType.DMA((KINDS, planes)),
        ],
        compiler_params=pltpu.CompilerParams(
            collective_id=0, has_side_effects=True, vmem_limit_bytes=60 * 1024 * 1024
        ),
        name="relay_attention",
    )(queries, keys, values)


def solution(mesh):
    spec = P(("seq", "head"), None)
    return jax.shard_map(
        per_device, mesh=mesh, in_specs=(spec, spec, spec), out_specs=spec, check_vma=False
    )
```

time: 113 us -> 37.5 us (0.33)
  the two profiles are of different devices: /device:TPU:28 before, /device:TPU:25 now
where the time goes in v1:
time: 37.5 us; the launch traced here: 37.3 us
  Pallas kernels  35.4 us (94%)
  local copies, waits for them, and re-layouts  1.87 us (5%)
    pallas_call x1, Pallas kernels, per_device(): pl.pallas_call(functools.partial(kernel, n_head, planes), out_shape=jax.S...  35.4 us
    unnamed x1, local copies, waits for them, and re-layouts  1.87 us

profile of v1, /device:TPU:25, one launch (start us, length us, event | category | flops | bytes accessed | tf_op | source)
XLA Modules:
  0.0 37.3 jit_solution(4850487075093020714)
XLA Ops:
  0.0 35.4 %relay_attention.1 = bf16[64,4096]{1,0:T(8,128)(2,1)} custom-call(bf16[64,4096]{1,0:T(8,128)(2,1)} %q_hbm.1, bf16[64,512]{1,0:T(8,128)(2,1)} %k_hbm.1, bf16[64,512]{1,0:T(8,128)(2,1)} %v_hbm.1), custom_call_target="tpu_custom_call" | custom-call | tf_op jit(solution)/shard_map/relay_attention/pallas_call | solution.py:216
  35.5 1.9 %copy.5 = bf16[64,4096]{1,0:T(8,128)(2,1)} copy(bf16[64,4096]{1,0:T(8,128)(2,1)} %relay_attention.1) | data formatting | bytes 1048576

commit v2 on v1

--- a/solution.py
+++ b/solution.py
@@ -13,7 +13,7 @@
 DH = 128
 GROUP = H // KV
 PLANE = 8
-Z, X, Y, DK, DV, C0 = 0, 1, 2, 3, 4, 5
+Z, X, Y, DK, DV, C0 = 0, 2, 4, 6, 7, 8
 KINDS = C0 + 4
 
 
@@ -77,8 +77,8 @@
             device_id_type=pl.DeviceIdType.MESH,
         )
 
-    def out_z(k):
-        return copy(Z, k, up, slot(k, y, x, core), later=1)
+    def out_z(k, half):
+        return copy(Z + half, k, up, slot(k, y, x, core), half, later=1)
 
     def outs(k):
         mine, xs, ys, diag = (
@@ -88,54 +88,37 @@
             slot(k, 1 - y, 1 - x, core),
         )
         return dict(
-            x=lambda: copy(X, k, to_x, mine),
-            y=lambda: copy(Y, k, to_y, mine),
+            xk=lambda: copy(X, k, to_x, mine, 0),
+            xv=lambda: copy(X + 1, k, to_x, mine, 1),
+            yk=lambda: copy(Y, k, to_y, mine, 0),
+            yv=lambda: copy(Y + 1, k, to_y, mine, 1),
+            dk=lambda: copy(DK, k, to_y, xs, 0),
+            dv=lambda: copy(DV, k, to_x, ys, 1),
             c0=lambda: copy(C0, k, to_core, mine),
-            dk=lambda: copy(DK, k, to_y, xs, 0),
             c1=lambda: copy(C0 + 1, k, to_core, xs),
-            dv=lambda: copy(DV, k, to_x, ys, 1),
             c2=lambda: copy(C0 + 2, k, to_core, ys),
             c3=lambda: copy(C0 + 3, k, to_core, diag),
         )
 
-    def ins(k):
-        def landed(kind, block, half=None):
-            copy(kind, k, to_x, block, half).wait_recv()
-
-        other = 1 - core
-        return dict(
-            z=lambda: landed(Z, slot(k, y, x, core)),
-            x=lambda: landed(X, slot(k, y, 1 - x, core)),
-            y=lambda: landed(Y, slot(k, 1 - y, x, core)),
-            dk=lambda: landed(DK, slot(k, 1 - y, 1 - x, core), 0),
-            dv=lambda: landed(DV, slot(k, 1 - y, 1 - x, core), 1),
-            c0=lambda: landed(C0, slot(k, y, x, other)),
-            c1=lambda: landed(C0 + 1, slot(k, y, 1 - x, other)),
-            c2=lambda: landed(C0 + 2, slot(k, 1 - y, x, other)),
-            c3=lambda: landed(C0 + 3, slot(k, 1 - y, 1 - x, other)),
-        )
-
-    def launch(k):
-        o = outs(k)
-
+    def landed(kind, k, block, half=None):
+        copy(kind, k, to_x, block, half).wait_recv()
+
+    def send_up(k, half):
         @pl.when(z < planes - 1)
         def _():
-            out_z(k).start()
-
-        o["x"]().start()
-        o["y"]().start()
-        o["c0"]().start()
+            out_z(k, half).start()
 
     scale = math.log2(math.e) / math.sqrt(DH)
-    width = PLANE * tok
     rows = GROUP * tok
 
-    def chunk(k, first):
-        base = (z - k) * PLANE
-        for g in range(KV):
+    def chunk(k, first, heads=range(KV), side=None):
+        blocks = PLANE if side is None else PLANE // 2
+        base = (z - k) * PLANE + (0 if side is None else side * blocks)
+        width = blocks * tok
+        for g in heads:
             cols = slice(g * DH, (g + 1) * DH)
-            kk = kv[pl.ds(base, PLANE), 0, :, cols].reshape(width, DH)
-            vv = kv[pl.ds(base, PLANE), 1, :, cols].reshape(width, DH)
+            kk = kv[pl.ds(base, blocks), 0, :, cols].reshape(width, DH)
+            vv = kv[pl.ds(base, blocks), 1, :, cols].reshape(width, DH)
             vv = jnp.concatenate([vv, jnp.ones_like(vv)], axis=1)
             qq = jnp.concatenate(
                 [q[:, (g * GROUP + h) * DH : (g * GROUP + h + 1) * DH] for h in range(GROUP)], axis=0
@@ -158,36 +141,94 @@
             acc[g] = pv
             mx[g] = jnp.broadcast_to(top, (rows, DH))
 
-    def step(k, first):
-        i, o = ins(k), outs(k)
-        i["x"]()
+    def relay_first(k):
+        o = outs(k)
+
+        @pl.when(k < z)
+        def _():
+            landed(Z, k + 1, slot(k + 1, y, x, core), 0)
+            send_up(k + 1, 0)
+            outs(k + 1)["xk"]().start()
+
+        landed(X, k, slot(k, y, 1 - x, core), 0)
         o["dk"]().start()
+        landed(Y + 1, k, slot(k, 1 - y, x, core), 1)
+        o["dv"]().start()
+
+    def relay_mid(k):
+        o = outs(k)
+
+        @pl.when(k < z)
+        def _():
+            landed(Z + 1, k + 1, slot(k + 1, y, x, core), 1)
+            send_up(k + 1, 1)
+            later = outs(k + 1)
+            later["yv"]().start()
+            later["xv"]().start()
+            later["yk"]().start()
+            later["c0"]().start()
+
+        landed(X + 1, k, slot(k, y, 1 - x, core), 1)
         o["c1"]().start()
-        i["y"]()
-        o["dv"]().start()
+        landed(Y, k, slot(k, 1 - y, x, core), 0)
         o["c2"]().start()
 
-        @pl.when(k < z)
-        def _():
-            ins(k + 1)["z"]()
-            launch(k + 1)
-
-        i["dk"]()
-        i["dv"]()
-        o["c3"]().start()
-        for name in ("c0", "c1", "c2", "c3"):
-            i[name]()
-        chunk(k, first)
-
-    launch(0)
+    def relay_second(k):
+        diag = slot(k, 1 - y, 1 - x, core)
+        landed(DK, k, diag, 0)
+        landed(DV, k, diag, 1)
+        outs(k)["c3"]().start()
+
+    def relay_near(k):
+        landed(C0, k, slot(k, y, x, 1 - core))
+        landed(C0 + 1, k, slot(k, y, 1 - x, 1 - core))
+
+    def relay_far(k):
+        landed(C0 + 2, k, slot(k, 1 - y, x, 1 - core))
+        landed(C0 + 3, k, slot(k, 1 - y, 1 - x, 1 - core))
+
+    o = outs(0)
+    for half in (0, 1):
+        send_up(0, half)
+    for name in ("xk", "yv", "xv", "yk", "c0"):
+        o[name]().start()
     own_q.wait()
-    step(0, True)
+    relay_first(0)
+    relay_mid(0)
+    relay_second(0)
+    relay_near(0)
+    relay_far(0)
+
+    @pl.when(z > 0)
+    def _():
+        relay_first(1)
+        chunk(0, True, (0, 1))
+        relay_mid(1)
+        chunk(0, True, (2, 3))
+        relay_second(1)
+
+    @pl.when(z == 0)
+    def _():
+        chunk(0, True)
 
     def body(k, carry):
-        step(k, False)
+        relay_near(k - 1)
+        relay_far(k - 1)
+        relay_first(k)
+        chunk(k - 1, False, (0, 1))
+        relay_mid(k)
+        chunk(k - 1, False, (2, 3))
+        relay_second(k)
         return carry
 
-    lax.fori_loop(1, z + 1, body, 0)
+    lax.fori_loop(2, z + 1, body, 0)
+
+    @pl.when(z > 0)
+    def _():
+        relay_near(z)
+        chunk(z, False, side=y)
+        relay_far(z)
+        chunk(z, False, side=1 - y)
 
     for g in range(KV):
         out = (acc[g, :, :DH] / acc[g, :, DH:]).astype(o_ref.dtype)
@@ -197,7 +238,8 @@
     def drain(k, carry):
         @pl.when(z < planes - 1)
         def _():
-            out_z(k).wait_send()
+            for half in (0, 1):
+                out_z(k, half).wait_send()
 
         for c in outs(k).values():
             c().wait_send()
@@ -215,7 +257,7 @@
     hbm = pl.BlockSpec(memory_space=pl.ANY)
     return pl.pallas_call(
         functools.partial(kernel, n_head, planes),
-        out_shape=jax.ShapeDtypeStruct(queries.shape, queries.dtype),
+        out_shape=pltpu.VMEM(queries.shape, queries.dtype),
         in_specs=[hbm] * 3,
         out_specs=pl.BlockSpec(memory_space=pltpu.VMEM),
         scratch_shapes=[

time: 37.5 us -> 34 us (0.907)
  Pallas kernels: 35.4 us -> 33.1 us
  local copies, waits for them, and re-layouts: 1.87 us -> 0.8 us
    pallas_call x1, Pallas kernels: 35.4 us -> 33.1 us  [per_device(): pl.pallas_call(functools.partial(kernel, n_head, planes), out_shape=pltpu...]
    unnamed x1, local copies, waits for them, and re-layouts: 1.87 us -> 0.8 us
where the time goes in v2:
time: 34 us; the launch traced here: 33.9 us
  Pallas kernels  33.1 us (97%)
  local copies, waits for them, and re-layouts  0.8 us (2%)
    pallas_call x1, Pallas kernels, per_device(): pl.pallas_call(functools.partial(kernel, n_head, planes), out_shape=pltpu...  33.1 us
    unnamed x1, local copies, waits for them, and re-layouts  0.8 us

profile of v2, /device:TPU:25, one launch (start us, length us, event | category | flops | bytes accessed | tf_op | source)
XLA Modules:
  0.0 33.9 jit_solution(9677865739287312259)
XLA Ops:
  0.0 33.1 %relay_attention.1 = bf16[64,4096]{1,0:T(8,128)(2,1)S(1)} custom-call(bf16[64,4096]{1,0:T(8,128)(2,1)} %q_hbm.1, bf16[64,512]{1,0:T(8,128)(2,1)} %k_hbm.1, bf16[64,512]{1,0:T(8,128)(2,1)} %v_hbm.1), custom_call_target="tpu_custom_call" | custom-call | tf_op jit(solution)/shard_map/relay_attention/pallas_call | solution.py:258
  33.1 0.8 %copy.5 = bf16[64,4096]{1,0:T(8,128)(2,1)} copy(bf16[64,4096]{1,0:T(8,128)(2,1)S(1)} %relay_attention.1) | data formatting | bytes 1048576

commit v3 on v2

--- a/solution.py
+++ b/solution.py
@@ -17,7 +17,7 @@
 KINDS = C0 + 4
 
 
-def kernel(n_head, planes, q_hbm, k_hbm, v_hbm, o_ref, kv, q, mx, acc, lsem, send, recv):
+def kernel(n_head, planes, q_hbm, k_hbm, v_hbm, o_ref, kv, q, mx, tot, acc, lsem, send, recv):
     tok = k_hbm.shape[0]
     me = lax.axis_index("seq") * n_head + lax.axis_index("head")
     core = lax.rem(me, 2)
@@ -119,27 +119,35 @@
             cols = slice(g * DH, (g + 1) * DH)
             kk = kv[pl.ds(base, blocks), 0, :, cols].reshape(width, DH)
             vv = kv[pl.ds(base, blocks), 1, :, cols].reshape(width, DH)
-            vv = jnp.concatenate([vv, jnp.ones_like(vv)], axis=1)
             qq = jnp.concatenate(
                 [q[:, (g * GROUP + h) * DH : (g * GROUP + h + 1) * DH] for h in range(GROUP)], axis=0
             )
             s = lax.dot_general(
-                qq, kk, (((1,), (1,)), ((), ())), preferred_element_type=jnp.float32
+                kk, qq, (((1,), (1,)), ((), ())), preferred_element_type=jnp.float32
             )
             if first:
-                row = lax.rem(lax.broadcasted_iota(jnp.int32, (rows, width), 0), tok)
-                col = lax.broadcasted_iota(jnp.int32, (rows, width), 1)
-                s = jnp.where(col <= row + lax.rem(me, PLANE) * tok, s, -jnp.inf)
-            top = jnp.max(s, axis=1, keepdims=True)
+                key = lax.broadcasted_iota(jnp.int32, (width, rows), 0)
+                row = lax.rem(lax.broadcasted_iota(jnp.int32, (width, rows), 1), tok)
+                s = jnp.where(key <= row + lax.rem(me, PLANE) * tok, s, -jnp.inf)
+            top = jnp.max(s, axis=0, keepdims=True)
             if not first:
-                old = mx[g, :, :1]
+                old = mx[g]
                 top = jnp.maximum(old, top)
-            p = jnp.exp2((s - top) * scale).astype(jnp.bfloat16)
-            pv = jnp.dot(p, vv, preferred_element_type=jnp.float32)
+            p = jnp.exp2((s - top) * scale)
+            total = jnp.sum(p, axis=0, keepdims=True)
+            pv = lax.dot_general(
+                vv,
+                p.astype(jnp.bfloat16),
+                (((0,), (0,)), ((), ())),
+                preferred_element_type=jnp.float32,
+            )
             if not first:
-                pv += acc[g] * jnp.exp2((old - top) * scale)
+                factor = jnp.exp2((old - top) * scale)
+                total += tot[g] * factor
+                pv += acc[g] * factor
             acc[g] = pv
-            mx[g] = jnp.broadcast_to(top, (rows, DH))
+            tot[g] = total
+            mx[g] = top
 
     def relay_first(k):
         o = outs(k)
@@ -231,7 +239,7 @@
         chunk(z, False, side=1 - y)
 
     for g in range(KV):
-        out = (acc[g, :, :DH] / acc[g, :, DH:]).astype(o_ref.dtype)
+        out = (acc[g] / tot[g]).T.astype(o_ref.dtype)
         for h in range(GROUP):
             o_ref[:, (g * GROUP + h) * DH : (g * GROUP + h + 1) * DH] = out[h * tok : (h + 1) * tok]
 
@@ -263,8 +271,9 @@
         scratch_shapes=[
             pltpu.VMEM((devices, 2, tok, KV * DH), jnp.bfloat16),
             pltpu.VMEM(queries.shape, jnp.bfloat16),
-            pltpu.VMEM((KV, rows, DH), jnp.float32),
-            pltpu.VMEM((KV, rows, 2 * DH), jnp.float32),
+            pltpu.VMEM((KV, 1, rows), jnp.float32),
+            pltpu.VMEM((KV, 1, rows), jnp.float32),
+            pltpu.VMEM((KV, DH, rows), jnp.float32),
             pltpu.SemaphoreType.DMA((3,)),
             pltpu.SemaphoreType.DMA((KINDS, planes)),
             pltpu.SemaphoreType.DMA((KINDS, planes)),

time: 34 us -> 31.1 us (0.915)
  Pallas kernels: 33.1 us -> 30.2 us
    pallas_call x1, Pallas kernels: 33.1 us -> 30.2 us  [per_device(): pl.pallas_call(functools.partial(kernel, n_head, planes), out_shape=pltpu...]
where the time goes in v3:
time: 31.1 us; the launch traced here: 31 us
  Pallas kernels  30.2 us (97%)
  local copies, waits for them, and re-layouts  0.8 us (3%)
    pallas_call x1, Pallas kernels, per_device(): pl.pallas_call(functools.partial(kernel, n_head, planes), out_shape=pltpu...  30.2 us
    unnamed x1, local copies, waits for them, and re-layouts  0.8 us

profile of v3, /device:TPU:25, one launch (start us, length us, event | category | flops | bytes accessed | tf_op | source)
XLA Modules:
  0.0 31.0 jit_solution(8974776782222454994)
XLA Ops:
  0.0 30.2 %relay_attention.1 = bf16[64,4096]{1,0:T(8,128)(2,1)S(1)} custom-call(bf16[64,4096]{1,0:T(8,128)(2,1)} %q_hbm.1, bf16[64,512]{1,0:T(8,128)(2,1)} %k_hbm.1, bf16[64,512]{1,0:T(8,128)(2,1)} %v_hbm.1), custom_call_target="tpu_custom_call" | custom-call | tf_op jit(solution)/shard_map/relay_attention/pallas_call | solution.py:266
  30.2 0.8 %copy.5 = bf16[64,4096]{1,0:T(8,128)(2,1)} copy(bf16[64,4096]{1,0:T(8,128)(2,1)S(1)} %relay_attention.1) | data formatting | bytes 1048576
